TPU v7x, 256 devices: a whole 4x4x8 slice. The times are simulated.
256 devices in a mesh: dp: 8 (over x, core), cls: 32 (over z, y).
Axes of the slice: x: 4, y: 4, z: 8, core: 2. Of those that a mesh axis runs over, the one named last changes fastest.
Arguments:
- centers: float32 [65536, 512], P('cls'), may hold values from -6 to 6
- momentum: float32 [65536, 512], P('cls'), may hold values from -6 to 6
- grad_rows: bfloat16 [1048576, 512], P(('dp', 'cls')), may hold values from -5400 to 5400
- row_ids: int32 [1048576], P(('dp', 'cls')), may hold values from -1 to 65535, as said below
Outputs:
- new_centers: float32 [65536, 512], P('cls')
- new_momentum: float32 [65536, 512], P('cls')
Inputs may be any that keep to these rules, and one draw needn't show every extreme that they name: `row_ids`: slots of one device come in 32 blocks of 128; block o holds only rows o * 2048 to (o + 1) * 2048 - 1 or -1; within a block the used slots come first, distinct and ascending, and one to 128 of them are used. In every draw, for some owner o, every device of some index of dp fills its whole block o.
All inputs are finite; a program needn't handle non-finite values.
Results may differ from a plain program's by a relative error of at most 0.0003.
Values may be sent and summed in bfloat16 or wider, within the bound.
A program may use at most 128 MiB of HBM per device.

v0:
```python
import math

import jax
import jax.numpy as jnp
from jax import lax
from jax.sharding import PartitionSpec as P

beta_decay = 0.9
learn_rate = 0.5
clip_rms = 1.0
eps_norm = 1e-06
eps_row = 1e-06


def padded_to(lines, peers):
    spare = -lines.shape[0] % peers
    if not spare:
        return lines
    return jnp.concatenate([lines, jnp.zeros((spare, *lines.shape[1:]), lines.dtype)])


def sum_by_parts(array, axis):
    lines = array.reshape(-1, *array.shape[1:][-1:])
    padded = padded_to(lines, lax.axis_size(axis))
    own = lax.psum_scatter(padded, axis, scatter_dimension=0, tiled=True)
    whole = lax.all_gather(own, axis, axis=0, tiled=True)
    return whole[: len(lines)].reshape(array.shape)


def from_everyone(array, axis):
    peers = lax.axis_size(axis)
    return lax.all_to_all(
        jnp.broadcast_to(array[None], (peers, *array.shape)), axis, 0, 0, tiled=True
    )


def of_everyone(array, axis):
    return from_everyone(array, axis).sum(axis=0)


def on_device(centers, momentum, grad_rows, row_ids):
    groups = lax.axis_size("cls")
    rows_dev = centers.shape[0]
    features = centers.shape[1]
    capacity = grad_rows.shape[0] // groups
    owner_of = lax.broadcasted_iota(jnp.int32, (groups, capacity), 0)
    sent_ids = row_ids.reshape(groups, capacity)
    local_ids = jnp.where(sent_ids >= 0, sent_ids - owner_of * rows_dev, -1)
    blocks = grad_rows.reshape(groups, capacity, features)
    got_rows, got_ids = (
        lax.all_to_all(blocks, "cls", split_axis=0, concat_axis=0, tiled=True),
        lax.all_to_all(local_ids, "cls", split_axis=0, concat_axis=0, tiled=True),
    )
    flat_rows = got_rows.reshape(groups * capacity, features)
    flat_ids = got_ids.reshape(groups * capacity)
    decayed = beta_decay * momentum
    onehot_rows = lax.broadcasted_iota(jnp.int32, (rows_dev, flat_ids.shape[0]), 0)
    table = (onehot_rows == flat_ids[None, :]).astype(jnp.bfloat16)
    partial_value = jnp.dot(table, flat_rows, preferred_element_type=jnp.float32)
    gradient = sum_by_parts(partial_value, "dp")
    squares = of_everyone(jnp.sum(gradient * gradient), "cls")
    ceiling = clip_rms * math.sqrt(rows_dev * groups * features)
    factor = jnp.minimum(1.0, ceiling / jnp.sqrt(squares + eps_norm))
    new_momentum = decayed + factor * gradient
    stepped = centers - learn_rate * new_momentum
    rescale = lax.rsqrt(jnp.mean(stepped * stepped, axis=1, keepdims=True) + eps_row)
    return (stepped * rescale, new_momentum)


def solution(mesh):
    placed = (P("cls", None), P("cls", None), P(("dp", "cls"), None), P(("dp", "cls")))
    return jax.shard_map(
        on_device,
        mesh=mesh,
        in_specs=placed,
        out_specs=(P("cls", None), P("cls", None)),
        check_vma=False,
    )
```

profile of v0, /device:TPU:1, one launch (start us, length us, event | category | flops | bytes accessed | tf_op | source)
XLA Modules:
  0.0 251.9 jit_solution(12827942257511966301)
XLA Ops:
  7.2 0.0 reduce-scatter.2.cloned.1.call-start
  7.2 0.8 compare_select_fusion
  8.0 20.4 %all_to_all.17 = s32[32,1,128]{2,1,0:T(1,128)S(1)} all-to-all(s32[32,1,128]{2,1,0:T(1,128)S(1)} %compare_select_fusion), channel_id=1, replica_groups=mesh['dp'=8,'cls'=32] {'cls'}, dimensions={0} | all-to-all | bytes 32768 | tf_op jit(solution)/shard_map/all_to_all | solution.py:52
  28.5 96.8 %all_to_all.18 = bf16[32,128,512]{2,1,0:T(8,128)(2,1)S(1)} all-to-all(bf16[32,128,512]{2,1,0:T(8,128)(2,1)} %bitcast.5), channel_id=1, replica_groups=mesh['dp'=8,'cls'=32] {'cls'}, dimensions={0} | all-to-all | bytes 8388608 | tf_op jit(solution)/shard_map/all_to_all | solution.py:51
  125.3 10.3 %fusion = f32[2048,512]{1,0:T(8,128)} fusion(bf16[4096,512]{1,0:T(8,128)(2,1)S(1)} %bitcast.6, s32[4096]{0:T(1024)S(1)} %bitcast.8), kind=kOutput, calls=%fused_computation.1 | convolution fusion | flops 8598323200 | bytes 8404992 | tf_op jit(solution)/shard_map/dot_general | solution.py:59
  135.6 0.0 reduce-scatter.2.cloned.1.call-update
  135.6 0.0 all-gather.2.cloned.1.call-start
  135.7 37.9 %reduce-scatter.2.cloned.1.call-done = f32[256,512]{1,0:T(8,128)} async-done(((f32[2048,512]{1,0:T(8,128)}), f32[256,512]{1,0:T(8,128)}) %reduce-scatter.2.cloned.1.call-update) | async-done | bytes 524304 | tf_op jit(solution)/shard_map/reduce_scatter | solution.py:25
  173.5 0.0 all-gather.2.cloned.1.call-update
  173.6 38.6 %all-gather.2.cloned.1.call-done = f32[2048,512]{1,0:T(8,128)} async-done(((f32[256,512]{1,0:T(8,128)}), f32[2048,512]{1,0:T(8,128)}) %all-gather.2.cloned.1.call-update) | async-done | bytes 4194320 | tf_op jit(solution)/shard_map/all_gather | solution.py:26
  212.1 3.9 %multiply_reduce_fusion.1 = f32[]{:T(128)} fusion(f32[2048,512]{1,0:T(8,128)} %all-gather.2.cloned.1.call-done), kind=kLoop, calls=%fused_computation.6 | loop fusion | flops 2097151 | bytes 4194308 | tf_op jit(solution)/shard_map/reduce_sum | solution.py:61
  216.0 0.7 broadcast_in_dim.12
  216.7 18.0 %all_to_all.19 = f32[32,1,1]{2,1,0:T(1,128)S(1)} all-to-all(f32[32,1,1]{2,1,0:T(1,128)S(1)} %broadcast_in_dim.12), channel_id=1, replica_groups=mesh['dp'=8,'cls'=32] {'cls'}, dimensions={0} | all-to-all | bytes 256 | tf_op jit(solution)/shard_map/all_to_all | solution.py:32
  234.7 0.6 reduce_sum.28
  236.0 0.0 copy-start
  236.0 5.8 %multiply_reduce_fusion = (f32[2048]{0:T(1024)S(1)}, f32[2048,512]{1,0:T(8,128)S(1)}) fusion(f32[2048,512]{1,0:T(8,128)} %param.4, f32[2048,512]{1,0:T(8,128)} %all-gather.2.cloned.1.call-done, f32[]{:T(128)S(6)} %min_shard_map.3, f32[2048,512]{1,0:T(8,128)} %param.5), kind=kLoop, calls=%fused_computation.3 | loop fusion | flops 7337984 | bytes 16785412 | tf_op jit(solution)/shard_map/reduce_sum | solution.py:66
  241.8 0.0 copy-start.1
  241.8 0.0 copy-done
  241.8 2.8 %broadcast_multiply_fusion = f32[2048,512]{1,0:T(8,128)} fusion(f32[2048]{0:T(1024)S(1)} %add_rsqrt_fusion, f32[2048,512]{1,0:T(8,128)S(1)} %copy-done, f32[2048,512]{1,0:T(8,128)S(1)} %get-tuple-element.3), kind=kLoop, calls=%fused_computation.7 | loop fusion | flops 3145728 | bytes 12591104 | tf_op jit(solution)/shard_map/mul | solution.py:67
  244.7 0.4 copy-done.1
  (2 shorter events, 0.0 us)
Async XLA Ops:
  7.2 166.4 %reduce-scatter.2.cloned.1.call-start = ((), (), s32[]{:S(2)}) async-start(), calls=%async_computation.4 | async-start | bytes 4718592 | tf_op jit(solution)/shard_map/reduce_scatter | solution.py:25
  135.6 76.5 %all-gather.2.cloned.1.call-start = ((), (), s32[]{:S(2)}) async-start(), calls=%async_computation.5 | async-start | bytes 4718592 | tf_op jit(solution)/shard_map/all_gather | solution.py:26
  236.0 5.9 %copy-start = (f32[2048,512]{1,0:T(8,128)S(1)}, f32[2048,512]{1,0:T(8,128)}, u32[]{:S(2)}) copy-start(f32[2048,512]{1,0:T(8,128)} %param.4) | copy-start | bytes 12582916
  241.8 3.3 %copy-start.1 = (f32[2048,512]{1,0:T(8,128)}, f32[2048,512]{1,0:T(8,128)S(1)}, u32[]{:S(2)}) copy-start(f32[2048,512]{1,0:T(8,128)S(1)} %get-tuple-element.3) | copy-start | bytes 12582916
Sparse Core Ops, SparseCore 0:
  135.7 37.7 reduce-scatter.1
  175.4 36.6 all-gather.1
where the time goes:
time: 252 us
  blocking collectives  135 us (54%)
  waiting for transfers between devices  76.5 us (30%)
  between operations  14.8 us (6%)
  other arithmetic  14 us (6%)
  matrix products  10.3 us (4%)
    all_to_all x1, blocking collectives, on_device(): lax.all_to_all(blocks, 'cls', split_axis=0, concat_axis=0, tiled=True)  96.8 us
    all_gather x1, waiting for transfers between devices, sum_by_parts(): whole = lax.all_gather(own, axis, axis=0, tiled=True)  38.6 us
    reduce_scatter x1, waiting for transfers between devices, sum_by_parts(): own = lax.psum_scatter(padded, axis, scatter_dimension=0, tiled=True)  37.9 us
    all_to_all x1, blocking collectives, on_device(): lax.all_to_all(local_ids, 'cls', split_axis=0, concat_axis=0, tiled=True)  20.4 us
    all_to_all x1, blocking collectives, from_everyone(): lax.all_to_all(jnp.broadcast_to(array[None], (peers, *array.shape)), axis...  18 us
    dot_general x1, matrix products, on_device(): jnp.dot(table, flat_rows, preferred_element_type=jnp.float32)  10.3 us
    reduce_sum x1, other arithmetic, on_device(): jnp.mean(stepped * stepped, axis=1, keepdims=True) + eps_row  5.82 us
  transfers between devices with their start and end apart: 2, of which 2 were waited for; matrix products, arithmetic and copies ran while one was open for 0% of the time, Pallas kernels for 0%

commit v1 on v0

v1 whole, which is shorter than its diff:
```python
import functools, math
import jax
import jax.numpy as jnp
from jax import lax
from jax.experimental import pallas as pl
from jax.experimental.pallas import tpu as pltpu
from jax.sharding import PartitionSpec as P

MESH = pl.DeviceIdType.MESH
NX, NY, NZ = 4, 4, 8
CAP, WIDE = 128, 128
ROWS = 2048
NCH = 4
CH = ROWS // NCH
HALF = CH // 2
OFFS = (0, 16, 48, 80, 112)
COUNT = (16, 32, 32, 32, 16)
beta_decay, learn_rate, clip_rms, eps_norm, eps_row = 0.9, 0.5, 1.0, 1e-06, 1e-06


def wrap(a, n):
    return lax.rem(a + n, n)


def kernel(rows, ids, g_out, sq_out, raw, idr, zs, zr, fp, dsw, sq1, sq2,
           raw_send, raw_recv, id_send, id_recv, z_send, z_recv, d_send, d_recv,
           a_send, a_recv, f_send, f_recv, s1_send, s1_recv, s2_send, s2_recv):
    d, g = lax.axis_index("dp"), lax.axis_index("cls")
    x, c = lax.div(d, 2), lax.rem(d, 2)
    z, y = lax.div(g, NY), lax.rem(g, NY)
    sgn = 1 - 2 * c
    other = 1 - c

    def dev(xx, cc, yy, zz):
        return (xx * 2 + cc, zz * NY + yy)

    bar = pltpu.get_barrier_semaphore()

    def greet_plane(j, _):
        cc, xx, yy = lax.rem(j, 2), lax.div(j, 8), lax.rem(lax.div(j, 2), NY)
        @pl.when(jnp.logical_or(jnp.logical_or(cc != c, xx != x), yy != y))
        def _():
            pl.semaphore_signal(bar, 1, device_id=dev(xx, cc, yy, z), device_id_type=MESH)
        return 0
    lax.fori_loop(0, 32, greet_plane, 0)

    def greet_z(j, _):
        pl.semaphore_signal(bar, 1, device_id=dev(x, c, y, wrap(z + j, NZ)), device_id_type=MESH)
        return 0
    lax.fori_loop(1, NZ, greet_z, 0)
    pl.semaphore_wait(bar, 31 + NZ - 1)

    me32 = (x * 2 + c) * NY + y

    def id_to(j, _):
        cc, xx, yy = lax.rem(j, 2), lax.div(j, 8), lax.rem(lax.div(j, 2), NY)
        @pl.when(jnp.logical_or(jnp.logical_or(cc != c, xx != x), yy != y))
        def _():
            pltpu.make_async_remote_copy(
                ids.at[:, yy], idr.at[me32], id_send, id_recv,
                device_id=dev(xx, cc, yy, z), device_id_type=MESH).start()
        return 0
    lax.fori_loop(0, 32, id_to, 0)
    pltpu.make_async_copy(ids.at[:, y], idr.at[me32], id_recv).start()

    def send_piece(p):
        k = 4 - p
        slot = OFFS[p] + (me32 if COUNT[p] == 32 else x * NY + y)

        def to(j, cc, zz):
            xx = lax.rem(x + lax.div(j, NY), NX)
            yy = lax.rem(y + lax.rem(j, NY), NY)
            src = rows.at[zz * NY + yy, :, pl.ds(pl.multiple_of(xx * WIDE, WIDE), WIDE)]
            return src, raw.at[slot], dev(xx, cc, yy, z)

        def remote(j, cc, zz):
            src, dst, who = to(j, cc, zz)
            pltpu.make_async_remote_copy(src, dst, raw_send.at[p], raw_recv.at[p],
                                         device_id=who, device_id_type=MESH).start()

        def mine(zz):
            src, dst, _ = to(0, c, zz)
            pltpu.make_async_copy(src, dst, raw_recv.at[p]).start()

        if COUNT[p] == 32:
            def body(j, _):
                remote(j, c, wrap(z + sgn * k, NZ))
                remote(j, other, wrap(z - sgn * k, NZ))
                return 0
            lax.fori_loop(1, NX * NY, body, 0)
            remote(0, other, wrap(z - sgn * k, NZ))
            mine(wrap(z + sgn * k, NZ))
        else:
            def body(j, _):
                remote(j, c, wrap(z + k, NZ))
                return 0
            lax.fori_loop(1, NX * NY, body, 0)
            mine(wrap(z + k, NZ))

    def all_in(ref, sem):
        pltpu.make_async_copy(ref, ref, sem).wait()

    def piece_in(p):
        all_in(raw.at[pl.ds(OFFS[p], COUNT[p])], raw_recv.at[p])

    def piece_out(p):
        all_in(raw.at[pl.ds(0, COUNT[p] - 1)], raw_send.at[p])

    def partial(p, r, out):
        k = 4 - p
        zz = wrap(z + sgn * k, NZ)
        base = (zz * NY + y) * ROWS + r * CH
        line = lax.broadcasted_iota(jnp.int32, (CH, 4 * CAP), 0) + base
        out[...] = jnp.zeros_like(out)

        def step(j, _):
            first = 4 * j if COUNT[p] == 32 else (2 * j + c) * NY
            who = jnp.concatenate([idr[first + t, zz] for t in range(4)], axis=1)
            hot = jnp.where(line == who, 1.0, 0.0).astype(jnp.bfloat16)
            lines = raw[pl.ds(OFFS[p] + 4 * j, 4)].reshape(4 * CAP, WIDE)
            out[...] += jnp.dot(hot, lines, preferred_element_type=jnp.float32)
            return 0
        lax.fori_loop(0, COUNT[p] // 4, step, 0)

    up = wrap(z + sgn, NZ)

    def z_copy(p, r):
        return pltpu.make_async_remote_copy(
            zs.at[p, r], zr.at[p, r], z_send.at[p, r], z_recv.at[p, r],
            device_id=dev(x, c, y, up), device_id_type=MESH)

    for p in range(2):
        send_piece(p)
    all_in(idr, id_recv)
    for p in range(4):
        if p + 2 < 5:
            send_piece(p + 2)
        piece_in(p)
        def chunk(r, _):
            partial(p, r, zs.at[p, r])
            if p:
                z_copy(p - 1, r).wait_recv()
                zs[p, r] = zs[p, r] + zr[p - 1, r]
            z_copy(p, r).start()
            return 0
        lax.fori_loop(0, NCH, chunk, 0)
    piece_in(4)

    mine_x = pl.ds(pl.multiple_of(x * WIDE, WIDE), WIDE)
    def last(r, _):
        partial(4, r, fp.at[r])
        return 0
    lax.fori_loop(0, NCH, last, 0)

    def d_copy(r):
        return pltpu.make_async_remote_copy(
            fp.at[r, pl.ds(pl.multiple_of(other * HALF, HALF), HALF)], dsw.at[r], d_send.at[r], d_recv.at[r],
            device_id=dev(x, other, y, z), device_id_type=MESH)

    def lines_of(r, cc):
        return pl.multiple_of(r * CH + cc * HALF, HALF)

    def a_copy(r, way, xx_slab, part, slot, step):
        to_x = wrap(x + 1 - 2 * way, NX)
        size = HALF // 2 if step else HALF
        at = lines_of(r, c) + (part * size if step else 0)
        ref = g_out.at[pl.ds(pl.multiple_of(at, size), size), pl.ds(pl.multiple_of(xx_slab * WIDE, WIDE), WIDE)]
        return pltpu.make_async_remote_copy(
            ref, ref, a_send.at[r, slot], a_recv.at[r, slot],
            device_id=dev(to_x, c, y, z), device_id_type=MESH)

    def f_copy(r, cc, slab, part, slot):
        size = HALF if part is None else HALF // 2
        at = lines_of(r, cc) + (0 if part is None else part * size)
        ref = g_out.at[pl.ds(pl.multiple_of(at, size), size), pl.ds(pl.multiple_of(slab * WIDE, WIDE), WIDE)]
        return pltpu.make_async_remote_copy(
            ref, ref, f_send.at[r, slot], f_recv.at[r, slot],
            device_id=dev(x, other, y, z), device_id_type=MESH)

    right, left, far = wrap(x + 1, NX), wrap(x - 1, NX), wrap(x + 2, NX)
    total = jnp.zeros((8, 128), jnp.float32)
    for t in range(NCH + 3):
        if t < NCH:
            r = t
            z_copy(3, r).wait_recv()
            fp[r] = fp[r] + zr[3, r]
            d_copy(r).start()
        if 0 <= t - 1 < NCH:
            r = t - 1
            d_copy(r).wait_recv()
            own = fp[r, pl.ds(pl.multiple_of(c * HALF, HALF), HALF)] + dsw[r]
            g_out[pl.ds(lines_of(r, c), HALF), mine_x] = own
            a_copy(r, 0, x, 0, 0, 0).start()
            a_copy(r, 1, x, 0, 1, 0).start()
            f_copy(r, c, x, None, 0).start()
            total = total + jnp.sum((own * own).reshape(HALF // 8, 8, 128), axis=0)
        if t == NCH:
            sq1[me32] = total

            def sq_to(j, _):
                cc, xx, yy = lax.rem(j, 2), lax.div(j, 8), lax.rem(lax.div(j, 2), NY)
                @pl.when(jnp.logical_or(jnp.logical_or(cc != c, xx != x), yy != y))
                def _():
                    pltpu.make_async_remote_copy(
                        sq1.at[me32], sq1.at[me32], s1_send, s1_recv,
                        device_id=dev(xx, cc, yy, z), device_id_type=MESH).start()
                return 0
            lax.fori_loop(0, 32, sq_to, 0)
        if 0 <= t - 2 < NCH:
            r = t - 2
            a_copy(r, 0, left, 0, 0, 0).wait_recv()
            f_copy(r, c, left, None, 1).start()
            a_copy(r, 0, left, 0, 2, 1).start()
            a_copy(r, 1, right, 0, 1, 0).wait_recv()
            f_copy(r, c, right, None, 2).start()
            a_copy(r, 1, right, 1, 3, 1).start()
        if 0 <= t - 3 < NCH:
            r = t - 3
            a_copy(r, 0, far, 0, 2, 1).wait_recv()
            f_copy(r, c, far, 0, 3).start()
            a_copy(r, 1, far, 1, 3, 1).wait_recv()
            f_copy(r, c, far, 1, 4).start()
        if t == NCH + 1:
            all_in(sq1.at[pl.ds(0, 31)], s1_recv)
            sq2[z] = jnp.sum(sq1[...], axis=0)

            def sq_up(j, _):
                pltpu.make_async_remote_copy(
                    sq2.at[z], sq2.at[z], s2_send, s2_recv,
                    device_id=dev(x, c, y, wrap(z + j, NZ)), device_id_type=MESH).start()
                return 0
            lax.fori_loop(1, NZ, sq_up, 0)
    all_in(sq2.at[pl.ds(0, NZ - 1)], s2_recv)
    sq_out[...] = jnp.sum(sq2[...], axis=0)
    for r in range(NCH):
        f_copy(r, other, x, None, 0).wait_recv()
        f_copy(r, other, left, None, 1).wait_recv()
        f_copy(r, other, right, None, 2).wait_recv()
        f_copy(r, other, far, 0, 3).wait_recv()
        f_copy(r, other, far, 1, 4).wait_recv()
    for r in range(NCH):
        d_copy(r).wait_send()
        for slot, step in ((0, 0), (1, 0), (2, 1), (3, 1)):
            a_copy(r, 0, x, 0, slot, step).wait_send()
        for slot, part in ((0, None), (1, None), (2, None), (3, 0), (4, 1)):
            f_copy(r, c, x, part, slot).wait_send()
    all_in(sq1.at[pl.ds(0, 31)], s1_send)
    all_in(sq2.at[pl.ds(0, NZ - 1)], s2_send)
    for p in range(5):
        piece_out(p)
    all_in(idr.at[pl.ds(0, 31)], id_send)
    def done(i, _):
        z_copy(lax.div(i, NCH), lax.rem(i, NCH)).wait_send()
        return 0
    lax.fori_loop(0, 4 * NCH, done, 0)


def exchange(rows, ids):
    dma = pltpu.SemaphoreType.DMA
    f32 = jnp.float32
    return pl.pallas_call(
        kernel,
        out_shape=(jax.ShapeDtypeStruct((ROWS, 512), f32), jax.ShapeDtypeStruct((8, 128), f32)),
        in_specs=[pl.BlockSpec(memory_space=pl.ANY), pl.BlockSpec(memory_space=pltpu.VMEM)],
        out_specs=(pl.BlockSpec(memory_space=pltpu.VMEM), pl.BlockSpec(memory_space=pltpu.VMEM)),
        scratch_shapes=[
            pltpu.VMEM((128, CAP, WIDE), jnp.bfloat16),
            pltpu.VMEM((32, NZ, 1, CAP), jnp.int32),
            pltpu.VMEM((4, NCH, CH, WIDE), f32),
            pltpu.VMEM((4, NCH, CH, WIDE), f32),
            pltpu.VMEM((NCH, CH, WIDE), f32),
            pltpu.VMEM((NCH, HALF, WIDE), f32),
            pltpu.VMEM((32, 8, 128), f32),
            pltpu.VMEM((NZ, 8, 128), f32),
            dma((5,)), dma((5,)), dma, dma,
            dma((4, NCH)), dma((4, NCH)), dma((NCH,)), dma((NCH,)),
            dma((NCH, 4)), dma((NCH, 4)), dma((NCH, 5)), dma((NCH, 5)),
            dma, dma, dma, dma,
        ],
        compiler_params=pltpu.CompilerParams(collective_id=0, has_side_effects=True,
                                             vmem_limit_bytes=50 * 2 ** 20),
        name="exchange",
    )(rows, ids)


def update_kernel(sq, g, m, cen, new_c, new_m):
    squares = jnp.sum(sq[...], keepdims=True)
    factor = jnp.minimum(1.0, clip_rms * math.sqrt(65536 * 512) / jnp.sqrt(squares + eps_norm))
    mom = beta_decay * m[...] + factor * g[...]
    new_m[...] = mom
    stepped = cen[...] - learn_rate * mom
    rescale = lax.rsqrt(jnp.mean(stepped * stepped, axis=1, keepdims=True) + eps_row)
    new_c[...] = stepped * rescale


def update(sq, g, m, cen):
    tile = 256
    spec = pl.BlockSpec((tile, 512), lambda i: (i, 0))
    shape = jax.ShapeDtypeStruct((ROWS, 512), jnp.float32)
    return pl.pallas_call(
        update_kernel,
        grid=(ROWS // tile,),
        out_shape=(shape, shape),
        in_specs=[pl.BlockSpec((8, 128), lambda i: (0, 0)), spec, spec, spec],
        out_specs=(spec, spec),
        name="update",
    )(sq, g, m, cen)


def on_device(centers, momentum, grad_rows, row_ids):
    g, sq = exchange(grad_rows.reshape(32, CAP, 512), row_ids.reshape(NZ, NY, 1, CAP))
    return update(sq, g, momentum, centers)


def solution(mesh):
    placed = (P("cls", None), P("cls", None), P(("dp", "cls"), None), P(("dp", "cls")))
    return jax.shard_map(
        on_device,
        mesh=mesh,
        in_specs=placed,
        out_specs=(P("cls", None), P("cls", None)),
        check_vma=False,
    )
```

time: 252 us -> 115 us (0.46)
  blocking collectives: 135 us -> 0 us
  Pallas kernels: 0 us -> 113 us
  waiting for transfers between devices: 76.5 us -> 0 us
  between operations: 14.8 us -> 0.65 us
  other arithmetic: 14 us -> 0 us
  matrix products: 10.3 us -> 0 us
    all_to_all x3 -> x0, blocking collectives: 135 us -> none  [the longest x1 96.8 us: on_device(): lax.all_to_all(blocks, 'cls', split_axis=0, concat_axis=0, tiled=True)]
    pallas_call x0 -> x2, Pallas kernels: none -> 113 us  [the longest x1 103 us: exchange(): pl.pallas_call(kernel, out_shape=(jax.ShapeDtypeStruct((ROWS, 512), f32),...]
    all_gather x1 -> x0, waiting for transfers between devices: 38.6 us -> none  [sum_by_parts(): whole = lax.all_gather(own, axis, axis=0, tiled=True)]
    reduce_scatter x1 -> x0, waiting for transfers between devices: 37.9 us -> none  [sum_by_parts(): own = lax.psum_scatter(padded, axis, scatter_dimension=0, tiled=True)]
    reduce_sum x3 -> x0, other arithmetic: 10.3 us -> none  [the longest x1 5.82 us: on_device(): jnp.mean(stepped * stepped, axis=1, keepdims=True) + eps_row]
    dot_general x1 -> x0, matrix products: 10.3 us -> none  [on_device(): jnp.dot(table, flat_rows, preferred_element_type=jnp.float32)]
    mul x2 -> x0, other arithmetic: 2.81 us -> none  [the longest x1 2.81 us: on_device(): return (stepped * rescale, new_momentum)]
  transfers between devices with their start and end apart: 2 -> 0, of which waited for: 2 -> 0; matrix products, arithmetic and copies ran while one was open for 0% -> 0% of each run, Pallas kernels for 0% -> 0%
where the time goes in v1:
time: 115 us
  Pallas kernels  113 us (98%)
  local copies, waits for them, and re-layouts  1.3 us (1%)
    pallas_call x1, Pallas kernels, exchange(): pl.pallas_call(kernel, out_shape=(jax.ShapeDtypeStruct((ROWS, 512), f32),...  103 us
    pallas_call x1, Pallas kernels, update(): pl.pallas_call(update_kernel, grid=(ROWS // tile,), out_shape=(shape, sha...  10.4 us

profile of v1, /device:TPU:1, one launch (start us, length us, event | category | flops | bytes accessed | tf_op | source)
XLA Modules:
  0.0 115.0 jit_solution(5935308710234942867)
XLA Ops:
  0.6 0.0 copy-start
  0.6 0.7 copy-done
  1.3 102.6 %exchange.1 = (f32[2048,512]{1,0:T(8,128)}, f32[8,128]{1,0:T(8,128)S(1)}) custom-call(bf16[32,128,512]{2,1,0:T(8,128)(2,1)} %bitcast.3, s32[8,4,1,128]{3,2,1,0:T(1,128)S(1)} %bitcast.2), custom_call_target="tpu_custom_call" | custom-call | tf_op jit(solution)/shard_map/exchange/pallas_call | solution.py:261
  104.0 0.0 copy-start.1
  104.0 0.6 copy-done.1
  104.6 10.4 %update.1 = (f32[2048,512]{1,0:T(8,128)}, f32[2048,512]{1,0:T(8,128)}) custom-call(f32[8,128]{1,0:T(8,128)} %copy-done.1, f32[2048,512]{1,0:T(8,128)} %get-tuple-element.5.g, f32[2048,512]{1,0:T(8,128)} %m.1, f32[2048,512]{1,0:T(8,128)} %cen.1), custom_call_target="tpu_custom_call" | custom-call | tf_op jit(solution)/shard_map/update/pallas_call | solution.py:300
Async XLA Ops:
  0.6 0.7 copy-start
  104.0 0.6 copy-start.1

commit v2 on v1

v2 whole, which is shorter than its diff:
```python
import functools, math
import jax
import jax.numpy as jnp
from jax import lax
from jax.experimental import pallas as pl
from jax.experimental.pallas import tpu as pltpu
from jax.sharding import PartitionSpec as P

MESH = pl.DeviceIdType.MESH
BF = jnp.bfloat16
NX, NY, NZ = 4, 4, 8
CAP, WIDE = 128, 128
ROWS = 2048
UNIT = NX * NY
HIGH = 4
LOW = ROWS // HIGH
NCH = 8
CH = ROWS // NCH
HALF = CH // 2
LAG_A, LAG_F, LAG_S = 3, 5, 3
TILE = 256
RING = 4
COUNT = (16, 32, 32, 32, 16)
UNITS = ((0,), (1, 2), (3, 4), (5, 6), (7,))
PIECE = (0, 1, 1, 2, 2, 3, 3, 4)
beta_decay, learn_rate, clip_rms, eps_norm, eps_row = 0.9, 0.5, 1.0, 1e-06, 1e-06


def wrap(a, n):
    return lax.rem(a + n, n)


def kernel(rows, ids, mom, cen, g_out, sq_out, mom_out, cen_out, raw, idr, hot, high, wide, zs, zr, fp, dsw, sq1, sq2,
           raw_send, raw_recv, id_send, id_recv, z_send, z_recv, d_send, d_recv,
           a_send, a_recv, f_send, f_recv, s1_send, s1_recv, s2_send, s2_recv, keep):
    d, g = lax.axis_index("dp"), lax.axis_index("cls")
    x, c = lax.div(d, 2), lax.rem(d, 2)
    z, y = lax.div(g, NY), lax.rem(g, NY)
    sgn = 1 - 2 * c
    other = 1 - c

    def dev(xx, cc, yy, zz):
        return (xx * 2 + cc, zz * NY + yy)

    bar = pltpu.get_barrier_semaphore()

    def greet_plane(j, _):
        cc, xx, yy = lax.rem(j, 2), lax.div(j, 8), lax.rem(lax.div(j, 2), NY)
        @pl.when(jnp.logical_or(jnp.logical_or(cc != c, xx != x), yy != y))
        def _():
            pl.semaphore_signal(bar, 1, device_id=dev(xx, cc, yy, z), device_id_type=MESH)
        return 0
    lax.fori_loop(0, 32, greet_plane, 0)

    def greet_z(j, _):
        pl.semaphore_signal(bar, 1, device_id=dev(x, c, y, wrap(z + j, NZ)), device_id_type=MESH)
        return 0
    lax.fori_loop(1, NZ, greet_z, 0)
    pl.semaphore_wait(bar, 31 + NZ - 1)

    me32 = c * UNIT + x * NY + y

    def place(t, dx):
        return t * 2 * NX + dx * 2 + c

    def id_round(t, _):
        for dx in range(NX):
            for cc in range(2):
                xx, yy = lax.rem(x + dx, NX), lax.rem(y + dx + t + c, NY)

                def send():
                    pltpu.make_async_remote_copy(
                        ids.at[:, yy], idr.at[place(t, dx)], id_send, id_recv,
                        device_id=dev(xx, cc, yy, z), device_id_type=MESH).start()
                if dx:
                    send()
                else:
                    pl.when(jnp.logical_or(yy != y, cc != c))(send)
        return 0
    lax.fori_loop(0, NY, id_round, 0)
    home = lax.rem(NY - c, NY)
    pltpu.make_async_copy(ids.at[:, y], idr.at[place(home, 0)], id_recv).start()

    def momentum_in():
        pltpu.make_async_copy(mom, mom_out, keep.at[0]).start()
        pltpu.make_async_copy(cen, cen_out, keep.at[1]).start()

    def send_piece(p):
        k = 4 - p
        full = COUNT[p] == 32
        near, away = wrap(z + (sgn if full else 1) * k, NZ), wrap(z - sgn * k, NZ)

        def where_to(t, dx):
            if full:
                unit = UNITS[p][0] + lax.div(t, 2)
                return unit, UNITS[p][0] * UNIT + place(t, dx)
            return UNITS[p][0], UNITS[p][0] * UNIT + t * NX + dx

        def lines(xx, yy, zz):
            return rows.at[zz * NY + yy, :, pl.ds(pl.multiple_of(xx * WIDE, WIDE), WIDE)]

        def remote(t, dx, xx, yy, cc, zz):
            unit, slot = where_to(t, dx)
            pltpu.make_async_remote_copy(lines(xx, yy, zz), raw.at[slot], raw_send.at[p], raw_recv.at[unit],
                                         device_id=dev(xx, cc, yy, z), device_id_type=MESH).start()

        def round_of(t, _):
            for dx in range(NX):
                xx, yy = lax.rem(x + dx, NX), lax.rem(y + dx + t + c, NY)

                def both():
                    remote(t, dx, xx, yy, c, near)
                    if full:
                        remote(t, dx, xx, yy, other, away)
                if dx:
                    both()
                else:
                    pl.when(yy != y)(both)
            return 0
        lax.fori_loop(0, NY, round_of, 0)
        if full:
            remote(home, 0, x, y, other, away)
        unit, slot = where_to(home, 0)
        pltpu.make_async_copy(lines(x, y, near), raw.at[slot], raw_recv.at[unit]).start()

    def all_in(ref, sem):
        pltpu.make_async_copy(ref, ref, sem).wait()

    def unit_in(u):
        all_in(raw.at[pl.ds(u * UNIT, UNIT)], raw_recv.at[u])

    def piece_out(p):
        all_in(raw.at[pl.ds(0, COUNT[p] - 1)], raw_send.at[p])

    def prepare(u):
        p = PIECE[u]
        zz = wrap(z + sgn * (4 - p), NZ)
        base = (zz * NY + y) * ROWS

        def local(b):
            at = 2 * b + c if COUNT[p] == 16 else (u + 1) % 2 * UNIT + b
            return idr[at, zz] - base

        def block(b, _):
            part = jnp.right_shift(local(b), LOW.bit_length() - 1).astype(jnp.float32)
            high[u % RING * UNIT + b] = jnp.broadcast_to(part, (CAP, WIDE)).T.astype(BF)
            return 0
        lax.fori_loop(0, UNIT, block, 0, unroll=4)
        line = lax.broadcasted_iota(jnp.int32, (LOW, 2 * CAP), 0)
        for q in range(UNIT // 2):
            low = jnp.bitwise_and(jnp.concatenate([local(2 * q), local(2 * q + 1)], axis=1), LOW - 1)
            hot[u % RING, :, q * 2 * CAP:(q + 1) * 2 * CAP] = jnp.where(line == low, 1.0, 0.0).astype(BF)

    def compute(u, out, add):
        for b in range(UNIT):
            lines, part = raw[u * UNIT + b], high[u % RING * UNIT + b]
            for h in range(HIGH):
                wide[b * CAP:(b + 1) * CAP, h * WIDE:(h + 1) * WIDE] = jnp.where(
                    part == jnp.asarray(h, BF), lines, jnp.zeros_like(lines))
        for n in range(HIGH // 2):
            v = jnp.dot(hot[u % RING], wide[:, 2 * n * WIDE:2 * (n + 1) * WIDE], preferred_element_type=jnp.float32)
            for q in range(2):
                at = pl.ds((2 * n + q) * LOW, LOW)
                now = v[:, q * WIDE:(q + 1) * WIDE]
                out[at, :] = out[at, :] + now if add else now

    up = wrap(z + sgn, NZ)

    def rows_at(r):
        return pl.ds(pl.multiple_of(r * CH, CH), CH)

    def z_copy(p, r):
        return pltpu.make_async_remote_copy(
            zs.at[p, rows_at(r)], zr.at[p, rows_at(r)], z_send.at[p, r], z_recv.at[p, r],
            device_id=dev(x, c, y, up), device_id_type=MESH)

    for p in range(2):
        send_piece(p)
    momentum_in()
    all_in(idr, id_recv)
    for u in range(3):
        prepare(u)
    for p in range(4):
        if p + 2 < 5:
            send_piece(p + 2)
        for u in UNITS[p]:
            unit_in(u)
            compute(u, zs.at[p], u != UNITS[p][0])

        def chunk(r, _):
            if p:
                z_copy(p - 1, r).wait_recv()
                zs[p, rows_at(r)] = zs[p, rows_at(r)] + zr[p - 1, rows_at(r)]
            z_copy(p, r).start()
            return 0
        lax.fori_loop(0, NCH, chunk, 0)
        for u in UNITS[p]:
            if u + 3 < 8:
                prepare(u + 3)
    unit_in(7)

    mine_x = pl.ds(pl.multiple_of(x * WIDE, WIDE), WIDE)
    compute(7, fp, False)

    def d_copy(r):
        return pltpu.make_async_remote_copy(
            fp.at[pl.ds(lines_of(r, other), HALF)], dsw.at[r], d_send.at[r], d_recv.at[r],
            device_id=dev(x, other, y, z), device_id_type=MESH)

    def lines_of(r, cc):
        return pl.multiple_of(r * CH + cc * HALF, HALF)

    def a_copy(r, way, xx_slab, part, slot, step):
        to_x = wrap(x + 1 - 2 * way, NX)
        size = HALF // 2 if step else HALF
        at = lines_of(r, c) + (part * size if step else 0)
        ref = g_out.at[pl.ds(pl.multiple_of(at, size), size), pl.ds(pl.multiple_of(xx_slab * WIDE, WIDE), WIDE)]
        return pltpu.make_async_remote_copy(
            ref, ref, a_send.at[r, slot], a_recv.at[r, slot],
            device_id=dev(to_x, c, y, z), device_id_type=MESH)

    def f_copy(r, cc, slab, part, slot):
        size = HALF if part is None else HALF // 2
        at = lines_of(r, cc) + (0 if part is None else part * size)
        ref = g_out.at[pl.ds(pl.multiple_of(at, size), size), pl.ds(pl.multiple_of(slab * WIDE, WIDE), WIDE)]
        return pltpu.make_async_remote_copy(
            ref, ref, f_send.at[r, slot], f_recv.at[r, slot],
            device_id=dev(x, other, y, z), device_id_type=MESH)

    right, left, far = wrap(x + 1, NX), wrap(x - 1, NX), wrap(x + 2, NX)
    total = jnp.zeros((8, 128), jnp.float32)
    for t in range(NCH + LAG_F):
        if t < NCH:
            r = t
            z_copy(3, r).wait_recv()
            fp[rows_at(r)] = fp[rows_at(r)] + zr[3, rows_at(r)]
            d_copy(r).start()
        if 0 <= t - 1 < NCH:
            r = t - 1
            d_copy(r).wait_recv()
            own = fp[pl.ds(lines_of(r, c), HALF)] + dsw[r]
            g_out[pl.ds(lines_of(r, c), HALF), mine_x] = own
            a_copy(r, 0, x, 0, 0, 0).start()
            a_copy(r, 1, x, 0, 1, 0).start()
            f_copy(r, c, x, None, 0).start()
            total = total + jnp.sum((own * own).reshape(HALF // 8, 8, 128), axis=0)
        if t == NCH:
            sq2[z] = total

            def sq_up(j, _):
                pltpu.make_async_remote_copy(
                    sq2.at[z], sq2.at[z], s2_send, s2_recv,
                    device_id=dev(x, c, y, wrap(z + j, NZ)), device_id_type=MESH).start()
                return 0
            lax.fori_loop(1, NZ, sq_up, 0)
        if 0 <= t - LAG_A < NCH:
            r = t - LAG_A
            a_copy(r, 0, left, 0, 0, 0).wait_recv()
            f_copy(r, c, left, None, 1).start()
            a_copy(r, 0, left, 0, 2, 1).start()
            a_copy(r, 1, right, 0, 1, 0).wait_recv()
            f_copy(r, c, right, None, 2).start()
            a_copy(r, 1, right, 1, 3, 1).start()
        if 0 <= t - LAG_F < NCH:
            r = t - LAG_F
            a_copy(r, 0, far, 0, 2, 1).wait_recv()
            f_copy(r, c, far, 0, 3).start()
            a_copy(r, 1, far, 1, 3, 1).wait_recv()
            f_copy(r, c, far, 1, 4).start()
        if t == NCH + LAG_S:
            all_in(sq2.at[pl.ds(0, NZ - 1)], s2_recv)
            sq1[me32] = jnp.sum(sq2[...], axis=0)

            def sq_to(j, _):
                cc, xx, yy = lax.rem(j, 2), lax.div(j, 8), lax.rem(lax.div(j, 2), NY)
                @pl.when(jnp.logical_or(jnp.logical_or(cc != c, xx != x), yy != y))
                def _():
                    pltpu.make_async_remote_copy(
                        sq1.at[me32], sq1.at[me32], s1_send, s1_recv,
                        device_id=dev(xx, cc, yy, z), device_id_type=MESH).start()
                return 0
            lax.fori_loop(0, 32, sq_to, 0)
    for r in range(NCH):
        f_copy(r, other, x, None, 0).wait_recv()
        f_copy(r, other, left, None, 1).wait_recv()
        f_copy(r, other, right, None, 2).wait_recv()
        f_copy(r, other, far, 0, 3).wait_recv()
        f_copy(r, other, far, 1, 4).wait_recv()
    all_in(sq1.at[pl.ds(0, 31)], s1_recv)
    sq_out[...] = jnp.sum(sq1[...], axis=0)
    for r in range(NCH):
        d_copy(r).wait_send()
        for slot, step in ((0, 0), (1, 0), (2, 1), (3, 1)):
            a_copy(r, 0, x, 0, slot, step).wait_send()
        for slot, part in ((0, None), (1, None), (2, None), (3, 0), (4, 1)):
            f_copy(r, c, x, part, slot).wait_send()
    all_in(sq1.at[pl.ds(0, 31)], s1_send)
    all_in(sq2.at[pl.ds(0, NZ - 1)], s2_send)
    pltpu.make_async_copy(mom, mom_out, keep.at[0]).wait()
    pltpu.make_async_copy(cen, cen_out, keep.at[1]).wait()
    for p in range(5):
        piece_out(p)
    all_in(idr.at[pl.ds(0, 31)], id_send)
    def done(i, _):
        z_copy(lax.div(i, NCH), lax.rem(i, NCH)).wait_send()
        return 0
    lax.fori_loop(0, 4 * NCH, done, 0)


def exchange(rows, ids, mom, cen):
    dma = pltpu.SemaphoreType.DMA
    f32 = jnp.float32
    table = jax.ShapeDtypeStruct((ROWS, 512), f32)
    return pl.pallas_call(
        kernel,
        out_shape=(table, jax.ShapeDtypeStruct((8, 128), f32), table, table),
        in_specs=[pl.BlockSpec(memory_space=pltpu.HBM)] * 4,
        out_specs=(pl.BlockSpec(memory_space=pltpu.VMEM),) * 4,
        scratch_shapes=[
            pltpu.VMEM((128, CAP, WIDE), jnp.bfloat16),
            pltpu.VMEM((32, NZ, 1, CAP), jnp.int32),
            pltpu.VMEM((RING, LOW, UNIT * CAP), BF),
            pltpu.VMEM((RING * UNIT, CAP, WIDE), BF),
            pltpu.VMEM((UNIT * CAP, HIGH * WIDE), BF),
            pltpu.VMEM((4, ROWS, WIDE), f32),
            pltpu.VMEM((4, ROWS, WIDE), f32),
            pltpu.VMEM((ROWS, WIDE), f32),
            pltpu.VMEM((NCH, HALF, WIDE), f32),
            pltpu.VMEM((32, 8, 128), f32),
            pltpu.VMEM((NZ, 8, 128), f32),
            dma((5,)), dma((8,)), dma, dma,
            dma((4, NCH)), dma((4, NCH)), dma((NCH,)), dma((NCH,)),
            dma((NCH, 4)), dma((NCH, 4)), dma((NCH, 5)), dma((NCH, 5)),
            dma, dma, dma, dma, dma((2,)),
        ],
        compiler_params=pltpu.CompilerParams(collective_id=0, has_side_effects=True,
                                             vmem_limit_bytes=40 * 2 ** 20),
        name="exchange",
    )(rows, ids, mom, cen)


def update_kernel(sq, g, m, cen, new_c, new_m):
    squares = jnp.sum(sq[...], keepdims=True)
    factor = jnp.minimum(1.0, clip_rms * math.sqrt(65536 * 512) / jnp.sqrt(squares + eps_norm))
    at = pl.ds(pl.multiple_of(pl.program_id(0) * TILE, TILE), TILE)
    mom = beta_decay * m[at] + factor * g[at]
    new_m[...] = mom
    stepped = cen[at] - learn_rate * mom
    rescale = lax.rsqrt(jnp.mean(stepped * stepped, axis=1, keepdims=True) + eps_row)
    new_c[...] = stepped * rescale


def update(sq, g, m, cen):
    spec = pl.BlockSpec((TILE, 512), lambda i: (i, 0))
    shape = jax.ShapeDtypeStruct((ROWS, 512), jnp.float32)
    return pl.pallas_call(
        update_kernel,
        grid=(ROWS // TILE,),
        out_shape=(shape, shape),
        in_specs=[pl.BlockSpec(memory_space=pltpu.VMEM)] * 4,
        out_specs=(spec, spec),
        compiler_params=pltpu.CompilerParams(vmem_limit_bytes=20 * 2 ** 20),
        name="update",
    )(sq, g, m, cen)


def on_device(centers, momentum, grad_rows, row_ids):
    g, sq, mom, cen = exchange(
        grad_rows.reshape(32, CAP, 512), row_ids.reshape(NZ, NY, 1, CAP), momentum, centers)
    return update(sq, g, mom, cen)


def solution(mesh):
    placed = (P("cls", None), P("cls", None), P(("dp", "cls"), None), P(("dp", "cls")))
    return jax.shard_map(
        on_device,
        mesh=mesh,
        in_specs=placed,
        out_specs=(P("cls", None), P("cls", None)),
        check_vma=False,
    )
```

time: 115 us -> 102 us (0.89)
  Pallas kernels: 113 us -> 101 us
    pallas_call x2, Pallas kernels: 113 us -> 101 us  [the longest x1 95.3 us: exchange(): pl.pallas_call(kernel, out_shape=(table, jax.ShapeDtypeStruct((8, 128), f...]
where the time goes in v2:
time: 102 us
  Pallas kernels  101 us (99%)
    pallas_call x1, Pallas kernels, exchange(): pl.pallas_call(kernel, out_shape=(table, jax.ShapeDtypeStruct((8, 128), f...  95.3 us
    pallas_call x1, Pallas kernels, update(): pl.pallas_call(update_kernel, grid=(ROWS // TILE,), out_shape=(shape, sha...  5.29 us

profile of v2, /device:TPU:1, one launch (start us, length us, event | category | flops | bytes accessed | tf_op | source)
XLA Modules:
  0.0 101.9 jit_solution(5901368100730591084)
XLA Ops:
  0.6 0.0 copy-start
  0.6 0.7 copy-done
  1.3 95.3 %exchange.1 = (f32[2048,512]{1,0:T(8,128)S(1)}, f32[8,128]{1,0:T(8,128)S(1)}, f32[2048,512]{1,0:T(8,128)S(1)}, f32[2048,512]{1,0:T(8,128)S(1)}) custom-call(bf16[32,128,512]{2,1,0:T(8,128)(2,1)} %bitcast.3, s32[8,4,1,128]{3,2,1,0:T(1,128)S(1)} %bitcast.2, f32[2048,512]{1,0:T(8,128)} %mom.1, f32[2048,512]{1,0:T(8,128)} %cen.1), custom_call_target="tpu_custom_call" | custom-call | tf_op jit(solution)/shard_map/exchange/pallas_call | solution.py:314
  96.7 5.3 %update.1 = (f32[2048,512]{1,0:T(8,128)}, f32[2048,512]{1,0:T(8,128)}) custom-call(f32[8,128]{1,0:T(8,128)S(1)} %get-tuple-element.6.sq, f32[2048,512]{1,0:T(8,128)S(1)} %get-tuple-element.7.g, f32[2048,512]{1,0:T(8,128)S(1)} %get-tuple-element.8.m, f32[2048,512]{1,0:T(8,128)S(1)} %get-tuple-element.9.cen), custom_call_target="tpu_custom_call" | custom-call | tf_op jit(solution)/shard_map/update/pallas_call | solution.py:356
Async XLA Ops:
  0.6 0.7 copy-start

commit v3 on v2

--- a/solution.py
+++ b/solution.py
@@ -17,8 +17,8 @@
 NCH = 8
 CH = ROWS // NCH
 HALF = CH // 2
-LAG_A, LAG_F, LAG_S = 3, 5, 3
-TILE = 256
+LAG_D, LAG_A, LAG_F, LAG_S = 2, 5, 9, 2
+TILE = 128
 RING = 4
 COUNT = (16, 32, 32, 32, 16)
 UNITS = ((0,), (1, 2), (3, 4), (5, 6), (7,))
@@ -235,8 +235,8 @@
             z_copy(3, r).wait_recv()
             fp[rows_at(r)] = fp[rows_at(r)] + zr[3, rows_at(r)]
             d_copy(r).start()
-        if 0 <= t - 1 < NCH:
-            r = t - 1
+        if 0 <= t - LAG_D < NCH:
+            r = t - LAG_D
             d_copy(r).wait_recv()
             own = fp[pl.ds(lines_of(r, c), HALF)] + dsw[r]
             g_out[pl.ds(lines_of(r, c), HALF), mine_x] = own
@@ -244,8 +244,8 @@
             a_copy(r, 1, x, 0, 1, 0).start()
             f_copy(r, c, x, None, 0).start()
             total = total + jnp.sum((own * own).reshape(HALF // 8, 8, 128), axis=0)
-        if t == NCH:
-            sq2[z] = total
+        if t == NCH - 1 + LAG_D:
+            sq2[z] = jnp.sum(total, axis=0, keepdims=True)
 
             def sq_up(j, _):
                 pltpu.make_async_remote_copy(
@@ -267,7 +267,7 @@
             f_copy(r, c, far, 0, 3).start()
             a_copy(r, 1, far, 1, 3, 1).wait_recv()
             f_copy(r, c, far, 1, 4).start()
-        if t == NCH + LAG_S:
+        if t == NCH - 1 + LAG_D + LAG_S:
             all_in(sq2.at[pl.ds(0, NZ - 1)], s2_recv)
             sq1[me32] = jnp.sum(sq2[...], axis=0)
 
@@ -313,7 +313,7 @@
     table = jax.ShapeDtypeStruct((ROWS, 512), f32)
     return pl.pallas_call(
         kernel,
-        out_shape=(table, jax.ShapeDtypeStruct((8, 128), f32), table, table),
+        out_shape=(table, jax.ShapeDtypeStruct((1, 128), f32), table, table),
         in_specs=[pl.BlockSpec(memory_space=pltpu.HBM)] * 4,
         out_specs=(pl.BlockSpec(memory_space=pltpu.VMEM),) * 4,
         scratch_shapes=[
@@ -326,8 +326,8 @@
             pltpu.VMEM((4, ROWS, WIDE), f32),
             pltpu.VMEM((ROWS, WIDE), f32),
             pltpu.VMEM((NCH, HALF, WIDE), f32),
-            pltpu.VMEM((32, 8, 128), f32),
-            pltpu.VMEM((NZ, 8, 128), f32),
+            pltpu.VMEM((32, 1, 128), f32),
+            pltpu.VMEM((NZ, 1, 128), f32),
             dma((5,)), dma((8,)), dma, dma,
             dma((4, NCH)), dma((4, NCH)), dma((NCH,)), dma((NCH,)),
             dma((NCH, 4)), dma((NCH, 4)), dma((NCH, 5)), dma((NCH, 5)),
@@ -339,27 +339,47 @@
     )(rows, ids, mom, cen)
 
 
-def update_kernel(sq, g, m, cen, new_c, new_m):
+def update_kernel(sq, g, m, cen, new_c, new_m, held_c, held_m, sent):
     squares = jnp.sum(sq[...], keepdims=True)
     factor = jnp.minimum(1.0, clip_rms * math.sqrt(65536 * 512) / jnp.sqrt(squares + eps_norm))
-    at = pl.ds(pl.multiple_of(pl.program_id(0) * TILE, TILE), TILE)
-    mom = beta_decay * m[at] + factor * g[at]
-    new_m[...] = mom
-    stepped = cen[at] - learn_rate * mom
-    rescale = lax.rsqrt(jnp.mean(stepped * stepped, axis=1, keepdims=True) + eps_row)
-    new_c[...] = stepped * rescale
+
+    def copies(i):
+        at = pl.ds(pl.multiple_of(i * TILE, TILE), TILE)
+        return (pltpu.make_async_copy(held_m.at[at], new_m.at[at], sent.at[0, i]),
+                pltpu.make_async_copy(held_c.at[at], new_c.at[at], sent.at[1, i]))
+
+    def tile(i, _):
+        at = pl.ds(pl.multiple_of(i * TILE, TILE), TILE)
+        mom = beta_decay * m[at] + factor * g[at]
+        held_m[at] = mom
+        stepped = cen[at] - learn_rate * mom
+        rescale = lax.rsqrt(jnp.mean(stepped * stepped, axis=1, keepdims=True) + eps_row)
+        held_c[at] = stepped * rescale
+        for copy in copies(i):
+            copy.start()
+        return 0
+    lax.fori_loop(0, ROWS // TILE, tile, 0)
+
+    def drain(i, _):
+        for copy in copies(i):
+            copy.wait()
+        return 0
+    lax.fori_loop(0, ROWS // TILE, drain, 0)
 
 
 def update(sq, g, m, cen):
-    spec = pl.BlockSpec((TILE, 512), lambda i: (i, 0))
     shape = jax.ShapeDtypeStruct((ROWS, 512), jnp.float32)
     return pl.pallas_call(
         update_kernel,
-        grid=(ROWS // TILE,),
         out_shape=(shape, shape),
         in_specs=[pl.BlockSpec(memory_space=pltpu.VMEM)] * 4,
-        out_specs=(spec, spec),
-        compiler_params=pltpu.CompilerParams(vmem_limit_bytes=20 * 2 ** 20),
+        out_specs=(pl.BlockSpec(memory_space=pltpu.HBM),) * 2,
+        scratch_shapes=[
+            pltpu.VMEM((ROWS, 512), jnp.float32),
+            pltpu.VMEM((ROWS, 512), jnp.float32),
+            pltpu.SemaphoreType.DMA((2, ROWS // TILE)),
+        ],
+        compiler_params=pltpu.CompilerParams(vmem_limit_bytes=24 * 2 ** 20),
         name="update",
     )(sq, g, m, cen)
 

time: 102 us -> 97.7 us (0.958)
  Pallas kernels: 101 us -> 96 us
    pallas_call x2, Pallas kernels: 101 us -> 96 us  [the longest x1 92.3 us: exchange(): pl.pallas_call(kernel, out_shape=(table, jax.ShapeDtypeStruct((1, 128), f...]
where the time goes in v3:
time: 97.7 us; the launch traced here: 97.5 us
  Pallas kernels  96 us (98%)
    pallas_call x1, Pallas kernels, exchange(): pl.pallas_call(kernel, out_shape=(table, jax.ShapeDtypeStruct((1, 128), f...  92.3 us
    pallas_call x1, Pallas kernels, update(): pl.pallas_call(update_kernel, out_shape=(shape, shape), in_specs=[pl.Bloc...  3.74 us

profile of v3, /device:TPU:1, one launch (start us, length us, event | category | flops | bytes accessed | tf_op | source)
XLA Modules:
  0.0 97.5 jit_solution(12847712852382336570)
XLA Ops:
  0.6 0.0 copy-start
  0.6 0.7 copy-done
  1.3 92.3 %exchange.1 = (f32[2048,512]{1,0:T(8,128)S(1)}, f32[1,128]{1,0:T(1,128)S(1)}, f32[2048,512]{1,0:T(8,128)S(1)}, f32[2048,512]{1,0:T(8,128)S(1)}) custom-call(bf16[32,128,512]{2,1,0:T(8,128)(2,1)} %bitcast.3, s32[8,4,1,128]{3,2,1,0:T(1,128)S(1)} %bitcast.2, f32[2048,512]{1,0:T(8,128)} %mom.1, f32[2048,512]{1,0:T(8,128)} %cen.1), custom_call_target="tpu_custom_call" | custom-call | tf_op jit(solution)/shard_map/exchange/pallas_call | solution.py:314
  93.6 3.7 %update.1 = (f32[2048,512]{1,0:T(8,128)}, f32[2048,512]{1,0:T(8,128)}) custom-call(f32[1,128]{1,0:T(1,128)S(1)} %get-tuple-element.6.sq, f32[2048,512]{1,0:T(8,128)S(1)} %get-tuple-element.7.g, f32[2048,512]{1,0:T(8,128)S(1)} %get-tuple-element.8.m, f32[2048,512]{1,0:T(8,128)S(1)} %get-tuple-element.9.cen), custom_call_target="tpu_custom_call" | custom-call | tf_op jit(solution)/shard_map/update/pallas_call | solution.py:372
Async XLA Ops:
  0.6 0.7 copy-start

commit v4 on v3

--- a/solution.py
+++ b/solution.py
@@ -30,9 +30,9 @@
     return lax.rem(a + n, n)
 
 
-def kernel(rows, ids, mom, cen, g_out, sq_out, mom_out, cen_out, raw, idr, hot, high, wide, zs, zr, fp, dsw, sq1, sq2,
+def kernel(rows, ids, mom, cen, g_out, sq_out, mom_out, cen_out, raw, idr, hot, high, wide, zs, zr, zsw, fp, dsw, sq1, sq2,
            raw_send, raw_recv, id_send, id_recv, z_send, z_recv, d_send, d_recv,
-           a_send, a_recv, f_send, f_recv, s1_send, s1_recv, s2_send, s2_recv, keep):
+           a_send, a_recv, f_send, f_recv, s1_send, s1_recv, s2_send, s2_recv, keep, t_send, t_recv):
     d, g = lax.axis_index("dp"), lax.axis_index("cls")
     x, c = lax.div(d, 2), lax.rem(d, 2)
     z, y = lax.div(g, NY), lax.rem(g, NY)
@@ -174,6 +174,11 @@
             zs.at[p, rows_at(r)], zr.at[p, rows_at(r)], z_send.at[p, r], z_recv.at[p, r],
             device_id=dev(x, c, y, up), device_id_type=MESH)
 
+    def trade():
+        return pltpu.make_async_remote_copy(
+            zs.at[0, pl.ds(pl.multiple_of(other * (ROWS // 2), ROWS // 2), ROWS // 2)], zsw,
+            t_send, t_recv, device_id=dev(x, other, y, z), device_id_type=MESH)
+
     for p in range(2):
         send_piece(p)
     momentum_in()
@@ -187,13 +192,35 @@
             unit_in(u)
             compute(u, zs.at[p], u != UNITS[p][0])
 
-        def chunk(r, _):
+        def fresh(i, _):
+            z_copy(p, other * (NCH // 2) + i).start()
+            return 0
+
+        def shared(i, _):
+            r = c * (NCH // 2) + i
             if p:
                 z_copy(p - 1, r).wait_recv()
                 zs[p, rows_at(r)] = zs[p, rows_at(r)] + zr[p - 1, rows_at(r)]
+            else:
+                zs[p, rows_at(r)] = zs[p, rows_at(r)] + zsw[rows_at(i)]
             z_copy(p, r).start()
             return 0
-        lax.fori_loop(0, NCH, chunk, 0)
+
+        def chunk(r, _):
+            z_copy(p - 1, r).wait_recv()
+            zs[p, rows_at(r)] = zs[p, rows_at(r)] + zr[p - 1, rows_at(r)]
+            z_copy(p, r).start()
+            return 0
+
+        if p == 0:
+            trade().start()
+            trade().wait_recv()
+        if p == 1:
+            lax.fori_loop(0, NCH // 2, fresh, 0)
+        if p < 2:
+            lax.fori_loop(0, NCH // 2, shared, 0)
+        else:
+            lax.fori_loop(0, NCH, chunk, 0)
         for u in UNITS[p]:
             if u + 3 < 8:
                 prepare(u + 3)
@@ -304,7 +331,13 @@
     def done(i, _):
         z_copy(lax.div(i, NCH), lax.rem(i, NCH)).wait_send()
         return 0
-    lax.fori_loop(0, 4 * NCH, done, 0)
+    lax.fori_loop(NCH, 4 * NCH, done, 0)
+
+    def done_first(i, _):
+        z_copy(0, c * (NCH // 2) + i).wait_send()
+        return 0
+    lax.fori_loop(0, NCH // 2, done_first, 0)
+    trade().wait_send()
 
 
 def exchange(rows, ids, mom, cen):
@@ -324,6 +357,7 @@
             pltpu.VMEM((UNIT * CAP, HIGH * WIDE), BF),
             pltpu.VMEM((4, ROWS, WIDE), f32),
             pltpu.VMEM((4, ROWS, WIDE), f32),
+            pltpu.VMEM((ROWS // 2, WIDE), f32),
             pltpu.VMEM((ROWS, WIDE), f32),
             pltpu.VMEM((NCH, HALF, WIDE), f32),
             pltpu.VMEM((32, 1, 128), f32),
@@ -331,7 +365,7 @@
             dma((5,)), dma((8,)), dma, dma,
             dma((4, NCH)), dma((4, NCH)), dma((NCH,)), dma((NCH,)),
             dma((NCH, 4)), dma((NCH, 4)), dma((NCH, 5)), dma((NCH, 5)),
-            dma, dma, dma, dma, dma((2,)),
+            dma, dma, dma, dma, dma((2,)), dma, dma,
         ],
         compiler_params=pltpu.CompilerParams(collective_id=0, has_side_effects=True,
                                              vmem_limit_bytes=40 * 2 ** 20),

time: 97.7 us -> 96.3 us (0.986)
  Pallas kernels: 96 us -> 94.6 us
    pallas_call x1, Pallas kernels: 92.3 us -> 90.9 us  [exchange(): pl.pallas_call(kernel, out_shape=(table, jax.ShapeDtypeStruct((1, 128), f...]
where the time goes in v4:
time: 96.3 us; the launch traced here: 96.1 us
  Pallas kernels  94.6 us (98%)
    pallas_call x1, Pallas kernels, exchange(): pl.pallas_call(kernel, out_shape=(table, jax.ShapeDtypeStruct((1, 128), f...  90.9 us
    pallas_call x1, Pallas kernels, update(): pl.pallas_call(update_kernel, out_shape=(shape, shape), in_specs=[pl.Bloc...  3.74 us

profile of v4, /device:TPU:1, one launch (start us, length us, event | category | flops | bytes accessed | tf_op | source)
XLA Modules:
  0.0 96.1 jit_solution(11013157054850209808)
XLA Ops:
  0.6 0.0 copy-start
  0.6 0.7 copy-done
  1.3 90.9 %exchange.1 = (f32[2048,512]{1,0:T(8,128)S(1)}, f32[1,128]{1,0:T(1,128)S(1)}, f32[2048,512]{1,0:T(8,128)S(1)}, f32[2048,512]{1,0:T(8,128)S(1)}) custom-call(bf16[32,128,512]{2,1,0:T(8,128)(2,1)} %bitcast.3, s32[8,4,1,128]{3,2,1,0:T(1,128)S(1)} %bitcast.2, f32[2048,512]{1,0:T(8,128)} %mom.1, f32[2048,512]{1,0:T(8,128)} %cen.1), custom_call_target="tpu_custom_call" | custom-call | tf_op jit(solution)/shard_map/exchange/pallas_call | solution.py:347
  92.2 3.7 %update.1 = (f32[2048,512]{1,0:T(8,128)}, f32[2048,512]{1,0:T(8,128)}) custom-call(f32[1,128]{1,0:T(1,128)S(1)} %get-tuple-element.6.sq, f32[2048,512]{1,0:T(8,128)S(1)} %get-tuple-element.7.g, f32[2048,512]{1,0:T(8,128)S(1)} %get-tuple-element.8.m, f32[2048,512]{1,0:T(8,128)S(1)} %get-tuple-element.9.cen), custom_call_target="tpu_custom_call" | custom-call | tf_op jit(solution)/shard_map/update/pallas_call | solution.py:406
Async XLA Ops:
  0.6 0.7 copy-start

commit v5 on v4

--- a/solution.py
+++ b/solution.py
@@ -17,7 +17,7 @@
 NCH = 8
 CH = ROWS // NCH
 HALF = CH // 2
-LAG_D, LAG_A, LAG_F, LAG_S = 2, 5, 9, 2
+LAG_D, LAG_A, LAG_F, LAG_S = 2, 6, 11, 2
 TILE = 128
 RING = 4
 COUNT = (16, 32, 32, 32, 16)

time: 96.3 us -> 95.9 us (level)
  no operation moved by 1% of the time
where the time goes in v5:
time: 95.9 us; the launch traced here: 95.7 us
  Pallas kernels  94.2 us (98%)
    pallas_call x1, Pallas kernels, exchange(): pl.pallas_call(kernel, out_shape=(table, jax.ShapeDtypeStruct((1, 128), f...  90.5 us
    pallas_call x1, Pallas kernels, update(): pl.pallas_call(update_kernel, out_shape=(shape, shape), in_specs=[pl.Bloc...  3.74 us

profile of v5, /device:TPU:1, one launch (start us, length us, event | category | flops | bytes accessed | tf_op | source)
XLA Modules:
  0.0 95.7 jit_solution(15145669770841436383)
XLA Ops:
  0.6 0.0 copy-start
  0.6 0.7 copy-done
  1.3 90.5 %exchange.1 = (f32[2048,512]{1,0:T(8,128)S(1)}, f32[1,128]{1,0:T(1,128)S(1)}, f32[2048,512]{1,0:T(8,128)S(1)}, f32[2048,512]{1,0:T(8,128)S(1)}) custom-call(bf16[32,128,512]{2,1,0:T(8,128)(2,1)} %bitcast.3, s32[8,4,1,128]{3,2,1,0:T(1,128)S(1)} %bitcast.2, f32[2048,512]{1,0:T(8,128)} %mom.1, f32[2048,512]{1,0:T(8,128)} %cen.1), custom_call_target="tpu_custom_call" | custom-call | tf_op jit(solution)/shard_map/exchange/pallas_call | solution.py:347
  91.8 3.7 %update.1 = (f32[2048,512]{1,0:T(8,128)}, f32[2048,512]{1,0:T(8,128)}) custom-call(f32[1,128]{1,0:T(1,128)S(1)} %get-tuple-element.6.sq, f32[2048,512]{1,0:T(8,128)S(1)} %get-tuple-element.7.g, f32[2048,512]{1,0:T(8,128)S(1)} %get-tuple-element.8.m, f32[2048,512]{1,0:T(8,128)S(1)} %get-tuple-element.9.cen), custom_call_target="tpu_custom_call" | custom-call | tf_op jit(solution)/shard_map/update/pallas_call | solution.py:406
Async XLA Ops:
  0.6 0.7 copy-start
